TPU v7x, 32 devices: a whole 2x2x4 slice. The times are simulated.
32 devices in a mesh: tp: 8 (over z, core), seq: 4 (over y, x).
Axes of the slice: x: 2, y: 2, z: 4, core: 2. Of those that a mesh axis runs over, the one named last changes fastest.
Arguments:
- residual: bfloat16 [1024, 4096], P('seq'), may hold values from -6 to 6
- mix_gain: float32 [4096], replicated, may hold values from 0.5 to 1.5
- in_proj: bfloat16 [4096, 4096], P(None, 'tp'), may hold values from -0.09375 to 0.09375
- branch_proj: bfloat16 [4096, 4096], P(None, 'tp'), may hold values from -0.09375 to 0.09375
- conv_weight: float32 [4, 4096], P(None, 'tp'), may hold values from -3 to 3
- conv_bias: float32 [4096], P('tp'), may hold values from -1.25 to 1.25
- input_gate: bfloat16 [16, 256, 256], P('tp'), may hold values from -0.375 to 0.375
- input_bias: float32 [4096], P('tp'), may hold values from -3 to 3
- decay_gate: bfloat16 [16, 256, 256], P('tp'), may hold values from -0.375 to 0.375
- decay_bias: float32 [4096], P('tp'), may hold values from -3 to 3
- decay_param: float32 [4096], P('tp'), may hold values from -13 to -2, as said below
- out_proj: bfloat16 [4096, 4096], P('tp'), may hold values from -0.25 to 0.25
- mlp_gain: float32 [4096], replicated, may hold values from 0.5 to 1.5
- gate_proj: bfloat16 [4096, 12288], P('seq', 'tp'), may hold values from -0.09375 to 0.09375
- up_proj: bfloat16 [4096, 12288], P('seq', 'tp'), may hold values from -0.09375 to 0.09375
- down_proj: bfloat16 [12288, 4096], P('tp'), may hold values from -0.078125 to 0.078125
Outputs:
- updated: bfloat16 [1024, 4096], P('seq')
Inputs may be any that keep to these rules, and one draw needn't show every extreme that they name: softplus(decay_param) lies between 0.02 / 1024 and 0.1 for every channel.
All inputs are finite; a program needn't handle non-finite values.
Results may differ from a plain program's by a relative error of at most 0.02.
Values may be sent and summed in bfloat16 or wider, within the bound.
A program may use at most 128 MiB of HBM per device.

v0:
```python
import jax
import jax.numpy as jnp
from jax import lax
from jax.sharding import PartitionSpec as P

epsilon = 1e-06


def from_behind(value, axis, steps):
    count = lax.axis_size(axis)
    leading, last = (max(0, -steps), min(count, count - steps))
    return lax.ppermute(value, axis, [(source, source + steps) for source in range(leading, last)])


def carried_in(shard, axis, combine, identity, reverse):
    count, mine = (lax.axis_size(axis), lax.axis_index(axis))
    everything = jax.tree.map(lambda part: lax.all_gather(part, axis), shard)
    start = jax.tree.map(
        lambda part, zero: jnp.broadcast_to(jnp.asarray(zero, part.dtype), part.shape),
        shard,
        identity,
    )

    def lap(k, before):
        at = count - 1 - k if reverse else k
        reached = at > mine if reverse else at < mine
        new = combine(before, jax.tree.map(lambda part: part[at], everything))
        return jax.tree.map(lambda a, b: jnp.where(reached, a, b), new, before)

    return lax.fori_loop(0, count, lap, start)


def summed_rows(product, extent, axis):
    everything = product(jnp.int32(0), lax.axis_size(axis) * extent)
    own = lax.psum_scatter(everything.astype(jnp.bfloat16), axis, scatter_dimension=0, tiled=True)
    return own.astype(jnp.float32)


def rms_norm(values, gain):
    wide = values.astype(jnp.float32)
    factor = lax.rsqrt(jnp.mean(wide * wide, axis=-1, keepdims=True) + epsilon)
    return (wide * factor * gain).astype(jnp.bfloat16)


def block_gates(values, weight, bias):
    heads, width = (weight.shape[0], weight.shape[1])
    grouped = values.reshape(values.shape[0], heads, width)
    mixed = jnp.einsum("thi,hij->thj", grouped, weight, preferred_element_type=jnp.float32)
    return jax.nn.sigmoid(mixed.reshape(values.shape[0], heads * width) + bias)


def smooth(inner, tail, conv_weight, conv_bias):
    taps = conv_weight.shape[0]
    length = inner.shape[0]
    padded = jnp.concatenate([tail, inner], axis=0).astype(jnp.float32)
    total = conv_bias + jnp.zeros((length, inner.shape[1]), jnp.float32)
    for offset in range(taps):
        total = total + conv_weight[offset] * padded[taps - 1 - offset : taps - 1 - offset + length]
    return lax.optimization_barrier(total.astype(jnp.bfloat16))


def combine_state(earlier, later):
    return (earlier[0] * later[0], later[0] * earlier[1] + later[1])


def channel_total(partial_value):
    return lax.psum(partial_value.astype(jnp.bfloat16), "tp").astype(jnp.float32)


def on_device(
    residual,
    mix_gain,
    in_proj,
    branch_proj,
    conv_weight,
    conv_bias,
    input_gate,
    input_bias,
    decay_gate,
    decay_bias,
    decay_param,
    out_proj,
    mlp_gain,
    gate_proj,
    up_proj,
    down_proj,
):
    length = residual.shape[0]
    taps = conv_weight.shape[0]
    normed = rms_norm(residual, mix_gain)
    branch = jax.nn.gelu(
        jnp.dot(normed, branch_proj, preferred_element_type=jnp.float32), approximate=True
    )
    inner = jnp.dot(normed, in_proj, preferred_element_type=jnp.float32).astype(jnp.bfloat16)
    tail = from_behind(inner[length - (taps - 1) :], "seq", 1)
    smoothed = smooth(inner, tail, conv_weight, conv_bias)
    input_rate = block_gates(smoothed, input_gate, input_bias)
    decay_rate = block_gates(smoothed, decay_gate, decay_bias)
    log_decay = -8.0 * decay_rate * jax.nn.softplus(decay_param)
    decay = jnp.exp(log_decay)
    position = lax.axis_index("seq")
    first = jnp.logical_and(position == 0, jnp.arange(length) == 0)[:, None]
    scale_in = jnp.where(first, 1.0, jnp.sqrt(-jnp.expm1(2.0 * log_decay)))
    pushed = smoothed.astype(jnp.float32) * input_rate * scale_in
    decays, partial_states = lax.associative_scan(combine_state, (decay, pushed), axis=0)
    end_decay = decays[-1]
    end_state = partial_states[-1]
    carried = carried_in(
        (end_decay, end_state),
        "seq",
        combine_state,
        (jnp.ones_like(end_decay), jnp.zeros_like(end_state)),
        False,
    )[1]
    states = partial_states + decays * carried[None]
    gated = (states * branch).astype(jnp.bfloat16)
    mixed = channel_total(jnp.dot(gated, out_proj, preferred_element_type=jnp.float32))
    middle = lax.optimization_barrier((residual.astype(jnp.float32) + mixed).astype(jnp.bfloat16))
    hidden_in = rms_norm(middle, mlp_gain)
    width = gate_proj.shape[1]
    columns = lax.all_to_all(hidden_in, "seq", split_axis=1, concat_axis=0, tiled=True)

    def term(start, count):
        block = lax.dynamic_slice_in_dim(columns, start, count, 0)
        return jnp.concatenate(
            [
                jnp.dot(block, gate_proj, preferred_element_type=jnp.float32),
                jnp.dot(block, up_proj, preferred_element_type=jnp.float32),
            ],
            axis=1,
        )

    joined = summed_rows(term, length, "seq")
    gate = joined[:, :width]
    up = joined[:, width:]
    hidden = (jax.nn.gelu(gate, approximate=True) * up).astype(jnp.bfloat16)
    output = channel_total(jnp.dot(hidden, down_proj, preferred_element_type=jnp.float32))
    return (middle.astype(jnp.float32) + output).astype(jnp.bfloat16)


def solution(mesh):
    in_specs = (
        P("seq", None),
        P(),
        P(None, "tp"),
        P(None, "tp"),
        P(None, "tp"),
        P("tp"),
        P("tp", None, None),
        P("tp"),
        P("tp", None, None),
        P("tp"),
        P("tp"),
        P("tp", None),
        P(),
        P("seq", "tp"),
        P("seq", "tp"),
        P("tp", None),
    )
    out_specs = P("seq", None)
    return jax.shard_map(
        on_device, mesh=mesh, in_specs=in_specs, out_specs=out_specs, check_vma=False
    )
```

profile of v0, /device:TPU:0, one launch (start us, length us, event | category | flops | bytes accessed | tf_op | source)
XLA Modules:
  0.0 392.3 jit_solution(13531175450782179382)
XLA Ops:
  6.5 2.2 fusion
  8.8 4.1 %convolution_convert_fusion.4 = bf16[256,512]{1,0:T(8,128)(2,1)S(1)} fusion(bf16[4096,512]{1,0:T(8,128)(2,1)} %param.20, bf16[256,4096]{1,0:T(8,128)(2,1)} %param.18, f32[4096]{0:T(1024)} %param.19, f32[256]{0:T(256)S(1)} %add_rsqrt_fusion.1), kind=kOutput, calls=%fused_computation.33 | convolution fusion | flops 1078067200 | bytes 6571008 | tf_op jit(solution)/shard_map/dot_general | solution.py:94
  13.0 4.9 %collective-permute-start = (bf16[3,512]{1,0:T(4,128)(2,1)S(1)}, bf16[3,512]{1,0:T(4,128)(2,1)S(1)}, u32[]{:S(2)}, u32[]{:S(2)}) collective-permute-start(bf16[3,512]{1,0:T(4,128)(2,1)S(1)} %slice.356), channel_id=1, source_target_pairs={{0,1},{1,2},{2,3},{4,5},{5,6},{6,7},{8,9},{9,10},{10,11},{12,13},{... | collective-permute-start | bytes 9224 | tf_op jit(solution)/shard_map/ppermute | solution.py:12
  18.0 1.2 collective-permute-done
  19.6 1.1 fusion.51
  20.6 2.1 copy.40
  22.7 2.0 fusion.53
  24.7 2.0 copy.39
  26.8 2.6 select_multiply_fusion
  29.4 0.8 copy-done.3
  30.1 2.5 slice.336
  32.7 2.5 slice.282
  35.1 2.5 slice.281
  37.6 0.7 slice.387
  38.3 2.5 slice.284
  40.8 2.5 slice.280
  43.3 2.5 slice.279
  45.8 1.3 multiply_add_fusion
  47.1 0.7 copy-done.4
  47.8 1.6 slice.334
  49.4 1.0 slice.288
  50.4 1.6 slice.287
  52.6 0.7 slice.290
  53.3 0.7 slice.286
  54.0 0.8 slice.285
  54.8 1.1 multiply_add_fusion.1
  62.4 0.8 fusion.66
  63.2 0.7 pad_maximum_fusion.8
  64.6 0.8 pad.123
  68.0 0.9 pad_maximum_fusion.5
  68.9 0.9 pad.109
  69.8 2.2 pad.125
  72.0 1.6 add.316
  74.2 1.7 fusion.63
  76.7 0.9 pad_maximum_fusion.3
  77.6 1.4 pad.110
  79.0 2.3 pad.111
  81.4 2.4 pad.127
  83.7 1.7 add.317
  85.4 1.8 add.308
  87.2 2.1 fusion.55
  89.3 0.7 pad_maximum_fusion.2
  90.1 2.6 pad.128
  92.7 1.7 pad_maximum_fusion.1
  94.3 2.6 pad.112
  97.0 2.6 pad.113
  99.6 0.7 add_bitcast_fusion
  100.3 9.8 %all-gather.1 = f32[4,1,512]{2,1,0:T(1,128)S(1)} all-gather(f32[1,1,512]{2,1,0:T(1,128)S(1)} %add_bitcast_fusion), channel_id=1, replica_groups=mesh['tp'=8,'seq'=4] {'seq'}, dimensions={0}, use_global_device_ids=true | all-gather | bytes 10240 | tf_op jit(solution)/shard_map/all_gather | solution.py:17
  110.1 1.7 pad.129
  111.8 0.7 add_bitcast_fusion.1
  112.5 7.2 %all-gather = f32[4,1,512]{2,1,0:T(1,128)S(1)} all-gather(f32[1,1,512]{2,1,0:T(1,128)S(1)} %add_bitcast_fusion.1), channel_id=1, replica_groups=mesh['tp'=8,'seq'=4] {'seq'}, dimensions={0}, use_global_device_ids=true | all-gather | bytes 10240 | tf_op jit(solution)/shard_map/all_gather | solution.py:17
  119.9 8.6 %convolution_convert_fusion.1 = bf16[256,4096]{1,0:T(8,128)(2,1)} fusion(bf16[512,4096]{1,0:T(8,128)(2,1)} %param.29, bf16[4096,512]{1,0:T(8,128)(2,1)} %param.21, bf16[256,4096]{1,0:T(8,128)(2,1)} %param.18, f32[4096]{0:T(1024)S(1)} %copy-done.18, f32[256]{0:T(256)S(1)} %copy-done.16, f32[256,512]{1,0:T(8,128)} %pad.128, f32[256,512]{1,0:T(8,128)} %pad.129, ...), kind=kOutput, calls=%fused_computation.11 | convolution fusion | flops 2154561536 | bytes 14699520 | tf_op jit(solution)/shard_map/dot_general | solution.py:117
  128.7 65.5 %all-reduce.35.cloned.1.call-done = bf16[256,4096]{1,0:T(8,128)(2,1)} async-done(((bf16[256,4096]{1,0:T(8,128)(2,1)}), bf16[256,4096]{1,0:T(8,128)(2,1)}) %all-reduce.35.cloned.1.call-update) | async-done | bytes 2097168 | tf_op jit(solution)/shard_map/psum | solution.py:67
  194.1 3.0 fusion.3
  197.7 0.7 fusion.6
  198.7 27.4 %all_to_all.19 = bf16[256,4,1024]{2,0,1:T(8,128)(2,1)S(1)} all-to-all(bf16[256,4,1024]{2,0,1:T(8,128)(2,1)S(1)} %bitcast.50), channel_id=1, replica_groups=mesh['tp'=8,'seq'=4] {'seq'}, dimensions={1} | all-to-all | bytes 4194304 | tf_op jit(solution)/shard_map/all_to_all | solution.py:121
  226.1 3.6 convolution_convert_fusion.2
  229.7 3.6 convolution_convert_fusion.3
  233.4 3.6 pad_maximum_fusion
  237.0 67.9 %reduce-scatter.2.cloned.1.call-done = bf16[256,3072]{1,0:T(8,128)(2,1)} async-done(((bf16[1024,3072]{1,0:T(8,128)(2,1)}), bf16[256,3072]{1,0:T(8,128)(2,1)}) %reduce-scatter.2.cloned.1.call-update) | async-done | bytes 1572880 | tf_op jit(solution)/shard_map/reduce_scatter | solution.py:35
  304.9 1.8 convert_element_type.66
  306.7 9.4 %convolution_convert_fusion = bf16[256,4096]{1,0:T(8,128)(2,1)} fusion(bf16[1536,4096]{1,0:T(8,128)(2,1)} %param.33, f32[256,3072]{1,0:T(8,128)S(1)} %convert_element_type.66), kind=kOutput, calls=%fused_computation.10 | convolution fusion | flops 3226206208 | bytes 17825792 | tf_op jit(solution)/shard_map/dot_general | solution.py:137
  316.1 65.3 %all-reduce.37.cloned.1.call-done = bf16[256,4096]{1,0:T(8,128)(2,1)} async-done(((bf16[256,4096]{1,0:T(8,128)(2,1)}), bf16[256,4096]{1,0:T(8,128)(2,1)}) %all-reduce.37.cloned.1.call-update) | async-done | bytes 2097168 | tf_op jit(solution)/shard_map/psum | solution.py:67
  381.4 4.3 %fusion.7 = bf16[256,4096]{1,0:T(8,128)(2,1)} fusion(bf16[256,4096]{1,0:T(8,128)(2,1)} %copy-done.2, bf16[256,4096]{1,0:T(8,128)(2,1)} %all-reduce.37.cloned.1.call-done), kind=kLoop, calls=%fused_computation.19 | loop fusion | flops 4194304 | bytes 6291456 | tf_op jit(solution)/shard_map/convert_element_type | solution.py:138
  (149 shorter events, 13.3 us)
Async XLA Ops:
  6.5 219.5 %copy-start = (bf16[1024,1536]{1,0:T(8,128)(2,1)S(1)}, bf16[1024,1536]{1,0:T(8,128)(2,1)}, u32[]{:S(2)}) copy-start(bf16[1024,1536]{1,0:T(8,128)(2,1)} %param.32) | copy-start | bytes 9437188
  6.5 187.6 %all-reduce.35.cloned.1.call-start = ((), (), s32[]{:S(2)}) async-start(), calls=%async_computation.2 | async-start | bytes 4194304 | tf_op jit(solution)/shard_map/psum | solution.py:67
  8.8 4.2 %copy-start.15 = (f32[256]{0:T(256)}, f32[256]{0:T(256)S(1)}, u32[]{:S(2)}) copy-start(f32[256]{0:T(256)S(1)} %add_rsqrt_fusion.1) | copy-start | bytes 3076
  8.8 9.1 %copy-start.13 = (f32[512]{0:T(512)S(1)}, f32[512]{0:T(512)}, u32[]{:S(2)}) copy-start(f32[512]{0:T(512)} %param.28) | copy-start | bytes 6148
  8.8 9.1 %copy-start.10 = (f32[4,512]{1,0:T(4,128)S(1)}, f32[4,512]{1,0:T(4,128)}, u32[]{:S(2)}) copy-start(f32[4,512]{1,0:T(4,128)} %param.22) | copy-start | bytes 24580
  8.8 10.5 %copy-start.14 = (f32[512]{0:T(512)S(1)}, f32[512]{0:T(512)}, u32[]{:S(2)}) copy-start(f32[512]{0:T(512)} %param.23) | copy-start | bytes 6148
  13.0 6.2 %collective-permute-start = (bf16[3,512]{1,0:T(4,128)(2,1)S(1)}, bf16[3,512]{1,0:T(4,128)(2,1)S(1)}, u32[]{:S(2)}, u32[]{:S(2)}) collective-permute-start(bf16[3,512]{1,0:T(4,128)(2,1)S(1)} %slice.356), channel_id=1, source_target_pairs={{0,1},{1,2},{2,3},{4,5},{5,6},{6,7},{8,9},{9,10},{10,11},{12,13},{... | collective-permute-start | bytes 9224 | tf_op jit(solution)/shard_map/ppermute | solution.py:12
  18.0 1.6 copy-start.6
  19.3 7.5 %copy-start.11 = (f32[512]{0:T(512)S(1)}, f32[512]{0:T(512)}, u32[]{:S(2)}) copy-start(f32[512]{0:T(512)} %param.25) | copy-start | bytes 6148
  19.3 7.5 %copy-start.12 = (f32[512]{0:T(512)S(1)}, f32[512]{0:T(512)}, u32[]{:S(2)}) copy-start(f32[512]{0:T(512)} %param.27) | copy-start | bytes 6148
  29.4 0.8 copy-start.3
  47.1 0.7 copy-start.4
  58.4 8.2 %copy-start.7 = (f32[31,512]{1,0:T(8,128)S(1)}, f32[31,512]{1,0:T(8,128)}, u32[]{:S(2)}) copy-start(f32[31,512]{1,0:T(8,128)} %slice.332) | copy-start | bytes 190468
  58.5 8.2 %copy-start.8 = (f32[31,512]{1,0:T(8,128)S(1)}, f32[31,512]{1,0:T(8,128)}, u32[]{:S(2)}) copy-start(f32[31,512]{1,0:T(8,128)} %slice.291) | copy-start | bytes 190468
  87.2 32.7 %copy-start.16 = (f32[256]{0:T(256)S(1)}, f32[256]{0:T(256)}, u32[]{:S(2)}) copy-start(f32[256]{0:T(256)} %copy-done.15) | copy-start | bytes 3076
  87.2 32.7 %copy-start.18 = (f32[4096]{0:T(1024)S(1)}, f32[4096]{0:T(1024)}, u32[]{:S(2)}) copy-start(f32[4096]{0:T(1024)} %param.19) | copy-start | bytes 49156
  89.3 20.8 %copy-start.5 = (f32[128,512]{1,0:T(8,128)S(1)}, f32[128,512]{1,0:T(8,128)}, u32[]{:S(2)}) copy-start(f32[128,512]{1,0:T(8,128)} %add.317) | copy-start | bytes 786436
  128.6 69.1 %copy-start.9 = (f32[4096]{0:T(1024)S(1)}, f32[4096]{0:T(1024)}, u32[]{:S(2)}) copy-start(f32[4096]{0:T(1024)} %param.30) | copy-start | bytes 49156
  128.6 176.3 %reduce-scatter.2.cloned.1.call-start = ((), (), s32[]{:S(2)}) async-start(), calls=%async_computation.3 | async-start | bytes 7864320 | tf_op jit(solution)/shard_map/reduce_scatter | solution.py:35
  197.1 1.3 copy-start.2
  226.1 3.6 copy-start.17
  237.0 144.5 %all-reduce.37.cloned.1.call-start = ((), (), s32[]{:S(2)}) async-start(), calls=%async_computation.4 | async-start | bytes 4194304 | tf_op jit(solution)/shard_map/psum | solution.py:67
  316.1 69.6 %copy-start.1 = (bf16[1024,1536]{1,0:T(8,128)(2,1)S(1)}, bf16[1024,1536]{1,0:T(8,128)(2,1)}, u32[]{:S(2)}) copy-start(bf16[1024,1536]{1,0:T(8,128)(2,1)} %param.32) | copy-start | bytes 9437188
Sparse Core Ops, SparseCore 0:
  128.7 65.3 all-reduce.34
  237.1 67.7 reduce-scatter.1
  316.3 65.1 all-reduce.36
where the time goes:
time: 394 us; the launch traced here: 392 us
  waiting for transfers between devices  200 us (51%)
  local copies, waits for them, and re-layouts  53.7 us (14%)
  blocking collectives  44.3 us (11%)
  other arithmetic  43 us (11%)
  matrix products  32.6 us (8%)
  between operations  13.7 us (3%)
  starting transfers between devices  4.96 us (1%)
    psum x2, waiting for transfers between devices, channel_total(): lax.psum(partial_value.astype(jnp.bfloat16), 'tp').astype(jnp.float32)  131 us
    reduce_scatter x1, waiting for transfers between devices, summed_rows(): lax.psum_scatter(everything.astype(jnp.bfloat16), axis, scatter_dimension...  67.9 us
    slice x52, local copies, waits for them, and re-layouts, on_device(): lax.associative_scan(combine_state, (decay, pushed), axis=0)  28 us
    all_to_all x1, blocking collectives, on_device(): lax.all_to_all(hidden_in, 'seq', split_axis=1, concat_axis=0, tiled=True)  27.4 us
    pad x28, local copies, waits for them, and re-layouts, on_device(): lax.associative_scan(combine_state, (decay, pushed), axis=0)  19.7 us
    all_gather x2, blocking collectives, carried_in(): everything = jax.tree.map(lambda part: lax.all_gather(part, axis), shard)  16.9 us
    dot_general x1, matrix products, on_device(): jnp.dot(hidden, down_proj, preferred_element_type=jnp.float32)  9.43 us
    dot_general x1, matrix products, on_device(): jnp.dot(gated, out_proj, preferred_element_type=jnp.float32)  8.64 us
  transfers between devices with their start and end apart: 4, of which 4 were waited for; matrix products, arithmetic and copies ran while one was open for 0% of the time, Pallas kernels for 0%

commit v1 on v0

--- a/solution.py
+++ b/solution.py
@@ -1,9 +1,19 @@
+import functools
 import jax
 import jax.numpy as jnp
 from jax import lax
 from jax.sharding import PartitionSpec as P
 
 epsilon = 1e-06
+
+
+def show_vectors_in(arr, axis_key):
+    big = lax.all_gather(arr, axis_key)
+    far_arr = jnp.sum(big, 0)
+    return far_arr
+
+
+measure_the_panels = functools.partial(show_vectors_in, axis_key="tp")
 
 
 def from_behind(value, axis, steps):
@@ -64,7 +74,7 @@
 
 
 def channel_total(partial_value):
-    return lax.psum(partial_value.astype(jnp.bfloat16), "tp").astype(jnp.float32)
+    return measure_the_panels(partial_value.astype(jnp.bfloat16)).astype(jnp.float32)
 
 
 def on_device(

time: 394 us -> 601 us (1.53)
  waiting for transfers between devices: 200 us -> 371 us
  other arithmetic: 43 us -> 65.3 us
  local copies, waits for them, and re-layouts: 53.7 us -> 62.4 us
    all_gather x0 -> x2, waiting for transfers between devices: none -> 302 us  [show_vectors_in(): big = lax.all_gather(arr, axis_key)]
    psum x2 -> x0, waiting for transfers between devices: 131 us -> none  [channel_total(): lax.psum(partial_value.astype(jnp.bfloat16), 'tp').astype(jnp.float32)]
    reduce_sum x0 -> x2, other arithmetic: none -> 21.1 us  [show_vectors_in(): far_arr = jnp.sum(big, 0)]
where the time goes in v1:
time: 601 us; the launch traced here: 599 us
  waiting for transfers between devices  371 us (62%)
  other arithmetic  65.3 us (11%)
  local copies, waits for them, and re-layouts  62.4 us (10%)
  blocking collectives  47.5 us (8%)
  matrix products  34.3 us (6%)
  between operations  13.7 us (2%)
    all_gather x2, waiting for transfers between devices, show_vectors_in(): big = lax.all_gather(arr, axis_key)  302 us
    reduce_scatter x1, waiting for transfers between devices, summed_rows(): lax.psum_scatter(everything.astype(jnp.bfloat16), axis, scatter_dimension...  66.9 us
    all_to_all x1, blocking collectives, on_device(): lax.all_to_all(hidden_in, 'seq', split_axis=1, concat_axis=0, tiled=True)  30.5 us
    slice x52, local copies, waits for them, and re-layouts, on_device(): lax.associative_scan(combine_state, (decay, pushed), axis=0)  28.1 us
    reduce_sum x2, other arithmetic, show_vectors_in(): far_arr = jnp.sum(big, 0)  21.1 us
    pad x28, local copies, waits for them, and re-layouts, on_device(): lax.associative_scan(combine_state, (decay, pushed), axis=0)  19.8 us
    all_gather x2, blocking collectives, carried_in(): everything = jax.tree.map(lambda part: lax.all_gather(part, axis), shard)  16.9 us
  transfers between devices with their start and end apart: 4, of which 4 were waited for; matrix products, arithmetic and copies ran while one was open for 0% of the time, Pallas kernels for 0%

profile of v1, /device:TPU:0, one launch (start us, length us, event | category | flops | bytes accessed | tf_op | source)
XLA Modules:
  0.0 599.1 jit_solution(10118021007132768531)
XLA Ops:
  6.5 2.2 fusion
  8.8 4.1 convolution_convert_fusion.4
  13.0 4.9 collective-permute-start
  18.0 1.2 collective-permute-done
  19.6 1.1 fusion.51
  20.6 2.1 copy.49
  22.7 2.0 fusion.53
  24.7 2.0 copy.48
  26.8 2.6 select_multiply_fusion
  29.4 0.8 copy-done.3
  30.2 2.5 slice.336
  32.7 2.5 slice.282
  35.2 2.5 slice.281
  38.4 2.5 slice.284
  40.9 2.5 slice.280
  43.4 2.5 slice.279
  45.9 1.3 multiply_add_fusion
  47.9 1.6 slice.334
  49.5 1.0 slice.288
  50.5 1.6 slice.287
  54.1 0.8 slice.285
  54.9 1.1 multiply_add_fusion.1
  62.5 0.8 fusion.66
  64.7 0.8 pad.123
  68.1 0.9 pad_maximum_fusion.5
  69.0 0.9 pad.109
  69.9 2.2 pad.125
  72.0 1.6 add.312
  74.3 1.7 fusion.63
  76.7 0.9 pad_maximum_fusion.3
  77.7 1.5 pad.110
  79.1 2.3 pad.111
  81.4 2.4 pad.127
  83.8 1.7 add.313
  85.5 1.8 add.304
  87.3 2.1 fusion.55
  89.4 0.7 pad_maximum_fusion.2
  90.1 2.6 pad.128
  92.8 1.7 pad_maximum_fusion.1
  94.4 2.6 pad.112
  97.1 2.6 pad.113
  99.7 0.7 add_bitcast_fusion
  100.4 9.8 %all-gather.3 = f32[4,1,512]{2,1,0:T(1,128)S(1)} all-gather(f32[1,1,512]{2,1,0:T(1,128)S(1)} %add_bitcast_fusion), channel_id=1, replica_groups=mesh['tp'=8,'seq'=4] {'seq'}, dimensions={0}, use_global_device_ids=true | all-gather | bytes 10240 | tf_op jit(solution)/shard_map/all_gather | solution.py:27
  110.2 1.7 pad.129
  111.9 0.7 add_bitcast_fusion.1
  112.6 7.2 %all-gather.2 = f32[4,1,512]{2,1,0:T(1,128)S(1)} all-gather(f32[1,1,512]{2,1,0:T(1,128)S(1)} %add_bitcast_fusion.1), channel_id=1, replica_groups=mesh['tp'=8,'seq'=4] {'seq'}, dimensions={0}, use_global_device_ids=true | all-gather | bytes 10240 | tf_op jit(solution)/shard_map/all_gather | solution.py:27
  120.0 8.6 %convolution_convert_fusion.1 = bf16[256,4096]{1,0:T(8,128)(2,1)} fusion(bf16[512,4096]{1,0:T(8,128)(2,1)} %param.29, bf16[4096,512]{1,0:T(8,128)(2,1)} %param.21, bf16[256,4096]{1,0:T(8,128)(2,1)} %param.18, f32[4096]{0:T(1024)S(1)} %copy-done.19, f32[256]{0:T(256)S(1)} %copy-done.17, f32[256,512]{1,0:T(8,128)} %pad.128, f32[256,512]{1,0:T(8,128)} %pad.129, ...), kind=kOutput, calls=%fused_computation.11 | convolution fusion | flops 2154561536 | bytes 14699520 | tf_op jit(solution)/shard_map/dot_general | solution.py:127
  128.9 151.3 %all-gather.7.cloned.1.call-done = bf16[2048,4096]{1,0:T(8,128)(2,1)} async-done(((bf16[256,4096]{1,0:T(8,128)(2,1)}), bf16[2048,4096]{1,0:T(8,128)(2,1)}) %all-gather.7.cloned.1.call-update) | async-done | bytes 16777232 | tf_op jit(solution)/shard_map/all_gather | solution.py:11
  280.2 10.5 %reduce_sum.43 = bf16[256,4096]{1,0:T(8,128)(2,1)} reduce(bf16[8,256,4096]{2,1,0:T(8,128)(2,1)} %bitcast.47, bf16[]{:T(256)} %constant.59.clone.1), dimensions={0}, to_apply=%region_3.4 | reduce | flops 7340032 | bytes 18874370 | tf_op jit(solution)/shard_map/reduce_sum | solution.py:12
  290.7 3.0 fusion.3
  294.2 0.8 copy-done.2
  295.0 2.0 fusion.6
  297.0 4.1 copy.44
  301.0 30.5 %all_to_all.19 = bf16[256,4,1024]{0,2,1:T(8,128)(2,1)} all-to-all(bf16[256,4,1024]{0,2,1:T(8,128)(2,1)} %bitcast.49), channel_id=1, replica_groups=mesh['tp'=8,'seq'=4] {'seq'}, dimensions={1} | all-to-all | bytes 4194304 | tf_op jit(solution)/shard_map/all_to_all | solution.py:131
  331.5 4.0 copy.45
  335.5 5.4 convolution_convert_fusion.2
  341.0 3.6 convolution_convert_fusion.3
  344.6 3.6 pad_maximum_fusion
  348.3 66.9 %reduce-scatter.2.cloned.1.call-done = bf16[256,3072]{1,0:T(8,128)(2,1)} async-done(((bf16[1024,3072]{1,0:T(8,128)(2,1)}), bf16[256,3072]{1,0:T(8,128)(2,1)}) %reduce-scatter.2.cloned.1.call-update) | async-done | bytes 1572880 | tf_op jit(solution)/shard_map/reduce_scatter | solution.py:45
  415.2 1.8 convert_element_type.70
  416.9 9.4 %convolution_convert_fusion = bf16[256,4096]{1,0:T(8,128)(2,1)} fusion(bf16[1536,4096]{1,0:T(8,128)(2,1)} %param.33, f32[256,3072]{1,0:T(8,128)S(1)} %convert_element_type.70), kind=kOutput, calls=%fused_computation.10 | convolution fusion | flops 3226206208 | bytes 17825792 | tf_op jit(solution)/shard_map/dot_general | solution.py:147
  426.4 151.2 %all-gather.9.cloned.1.call-done = bf16[2048,4096]{1,0:T(8,128)(2,1)} async-done(((bf16[256,4096]{1,0:T(8,128)(2,1)}), bf16[2048,4096]{1,0:T(8,128)(2,1)}) %all-gather.9.cloned.1.call-update) | async-done | bytes 16777232 | tf_op jit(solution)/shard_map/all_gather | solution.py:11
  577.6 10.6 %reduce_sum.45 = bf16[256,4096]{1,0:T(8,128)(2,1)} reduce(bf16[8,256,4096]{2,1,0:T(8,128)(2,1)} %bitcast.48, bf16[]{:T(256)} %constant.59.clone.1), dimensions={0}, to_apply=%region_6.7 | reduce | flops 7340032 | bytes 18874370 | tf_op jit(solution)/shard_map/reduce_sum | solution.py:12
  588.2 4.3 fusion.7
  (154 shorter events, 16.7 us)
Async XLA Ops:
  6.5 329.0 %copy-start = (bf16[1024,1536]{1,0:T(8,128)(2,1)S(1)}, bf16[1024,1536]{1,0:T(8,128)(2,1)}, u32[]{:S(2)}) copy-start(bf16[1024,1536]{1,0:T(8,128)(2,1)} %param.32) | copy-start | bytes 9437188
  6.5 273.6 %all-gather.7.cloned.1.call-start = ((), (), s32[]{:S(2)}) async-start(), calls=%async_computation.3 | async-start | bytes 18874368 | tf_op jit(solution)/shard_map/all_gather | solution.py:11
  8.8 4.2 copy-start.16
  8.8 9.1 %copy-start.14 = (f32[512]{0:T(512)S(1)}, f32[512]{0:T(512)}, u32[]{:S(2)}) copy-start(f32[512]{0:T(512)} %param.28) | copy-start | bytes 6148
  8.8 9.1 %copy-start.11 = (f32[4,512]{1,0:T(4,128)S(1)}, f32[4,512]{1,0:T(4,128)}, u32[]{:S(2)}) copy-start(f32[4,512]{1,0:T(4,128)} %param.22) | copy-start | bytes 24580
  8.8 10.5 %copy-start.15 = (f32[512]{0:T(512)S(1)}, f32[512]{0:T(512)}, u32[]{:S(2)}) copy-start(f32[512]{0:T(512)} %param.23) | copy-start | bytes 6148
  13.0 6.2 %collective-permute-start = (bf16[3,512]{1,0:T(4,128)(2,1)S(1)}, bf16[3,512]{1,0:T(4,128)(2,1)S(1)}, u32[]{:S(2)}, u32[]{:S(2)}) collective-permute-start(bf16[3,512]{1,0:T(4,128)(2,1)S(1)} %slice.356), channel_id=1, source_target_pairs={{0,1},{1,2},{2,3},{4,5},{5,6},{6,7},{8,9},{9,10},{10,11},{12,13},{... | collective-permute-start | bytes 9224 | tf_op jit(solution)/shard_map/ppermute | solution.py:22
  18.0 1.6 copy-start.7
  19.3 7.5 %copy-start.12 = (f32[512]{0:T(512)S(1)}, f32[512]{0:T(512)}, u32[]{:S(2)}) copy-start(f32[512]{0:T(512)} %param.25) | copy-start | bytes 6148
  19.3 7.5 %copy-start.13 = (f32[512]{0:T(512)S(1)}, f32[512]{0:T(512)}, u32[]{:S(2)}) copy-start(f32[512]{0:T(512)} %param.27) | copy-start | bytes 6148
  29.4 0.8 copy-start.3
  47.2 0.7 copy-start.5
  58.5 8.3 %copy-start.8 = (f32[31,512]{1,0:T(8,128)S(1)}, f32[31,512]{1,0:T(8,128)}, u32[]{:S(2)}) copy-start(f32[31,512]{1,0:T(8,128)} %slice.332) | copy-start | bytes 190468
  58.5 8.2 %copy-start.9 = (f32[31,512]{1,0:T(8,128)S(1)}, f32[31,512]{1,0:T(8,128)}, u32[]{:S(2)}) copy-start(f32[31,512]{1,0:T(8,128)} %slice.291) | copy-start | bytes 190468
  87.3 32.7 %copy-start.17 = (f32[256]{0:T(256)S(1)}, f32[256]{0:T(256)}, u32[]{:S(2)}) copy-start(f32[256]{0:T(256)} %copy-done.16) | copy-start | bytes 3076
  87.3 32.7 %copy-start.19 = (f32[4096]{0:T(1024)S(1)}, f32[4096]{0:T(1024)}, u32[]{:S(2)}) copy-start(f32[4096]{0:T(1024)} %param.19) | copy-start | bytes 49156
  89.4 20.8 %copy-start.6 = (f32[128,512]{1,0:T(8,128)S(1)}, f32[128,512]{1,0:T(8,128)}, u32[]{:S(2)}) copy-start(f32[128,512]{1,0:T(8,128)} %add.313) | copy-start | bytes 786436
  128.7 286.5 %reduce-scatter.2.cloned.1.call-start = ((), (), s32[]{:S(2)}) async-start(), calls=%async_computation.2 | async-start | bytes 7864320 | tf_op jit(solution)/shard_map/reduce_scatter | solution.py:45
  290.7 4.3 copy-start.10
  293.7 1.3 copy-start.2
  335.5 5.4 copy-start.4
  335.5 5.4 copy-start.18
  348.2 229.3 %all-gather.9.cloned.1.call-start = ((), (), s32[]{:S(2)}) async-start(), calls=%async_computation.4 | async-start | bytes 18874368 | tf_op jit(solution)/shard_map/all_gather | solution.py:11
  577.6 15.0 %copy-start.1 = (bf16[1024,1536]{1,0:T(8,128)(2,1)S(1)}, bf16[1024,1536]{1,0:T(8,128)(2,1)}, u32[]{:S(2)}) copy-start(bf16[1024,1536]{1,0:T(8,128)(2,1)} %param.32) | copy-start | bytes 9437188
Sparse Core Ops, SparseCore 0:
  128.8 151.3 all-gather.6
  348.4 66.7 reduce-scatter.1
  426.5 151.0 all-gather.8
